TPU v7x, 32 devices: a whole 2x2x4 slice. The times are simulated.
32 devices in a mesh: seq: 4 (over y, x), tp: 4 (over z), grp: 2 (over core).
Axes of the slice: x: 2, y: 2, z: 4, core: 2. Of those that a mesh axis runs over, the one named last changes fastest.
Arguments:
- queries: bfloat16 [4, 64, 128], P('grp', 'tp'), may hold values from -2000 to 2000
- cache_pool: bfloat16 [512, 8, 2, 128, 128], P(('seq', 'grp'), 'tp'), may hold values from -6 to 6
- block_scale: bfloat16 [512, 8, 2], P(('seq', 'grp'), 'tp'), may hold values from 0.29 to 3
- block_table: int32 [4, 128], replicated, may hold values from 0 to 511, as said below
- lengths: int32 [4], replicated, may hold values from 128 to 16384
- output_weight: bfloat16 [8192, 8192], P('tp', ('seq', 'grp')), may hold values from -0.0625 to 0.0625
Outputs:
- attention_output: bfloat16 [4, 8192], P('tp', ('seq', 'grp'))
- decode_cache: bfloat16 [4, 128, 8, 2, 128, 128], P('grp', 'seq', 'tp')
- decode_scale: bfloat16 [4, 128, 8, 2], P('grp', 'seq', 'tp')
Inputs may be any that keep to these rules, and one draw needn't show every extreme that they name: block_table names every pool slot exactly once. Take any run of 64 slots starting at a multiple of 64, any group of 2 consecutive requests starting at a multiple of 2, and any range of 32 block positions starting at a multiple of 32: exactly 8 slots of the run hold blocks of those requests at those positions.
All inputs are finite; a program needn't handle non-finite values.
Results may differ from a plain program's by a relative error of at most 0.014.
Values may be sent and summed in bfloat16 or wider, within the bound.
A program may use at most 64 MiB of HBM per device.

v0:
```python
import functools
import math

import jax
import jax.numpy as jnp
from jax import lax
from jax.experimental import pallas as pl
from jax.experimental.pallas import tpu as pltpu
from jax.sharding import PartitionSpec as P

MESH = pl.DeviceIdType.MESH
absent_score = -1e30
absent_limit = -1e29


def xor_index(index, mask):
    out = index
    bit = 1
    while bit <= mask:
        if mask & bit:
            out = out + bit - 2 * bit * ((index // bit) % 2)
        bit *= 2
    return out


def exchange_kernel(
    dims,
    lengths_in,
    table_in,
    block_scale_in,
    queries_in,
    pool_ref,
    weight_ref,
    placed_ref,
    scales_out_ref,
    output_ref,
    lengths_ref,
    table_ref,
    block_scale_ref,
    queries_ref,
    raw,
    send,
    arrived,
    weights,
    all_queries,
    scores,
    peaks,
    sums,
    accums,
    parts,
    parts_in,
    attended,
    projected,
    projected_in,
    scales_in,
    scales_wide,
    arrival_rows,
    pick_rows,
    scale_words,
    arrival_words,
    pick_words,
    load_sems,
    local_sems,
    word_sems,
    block_send,
    block_recv,
    query_send,
    query_recv,
    scale_send,
    scale_recv,
    part_send,
    part_recv,
    att_send,
    att_recv,
    proj_send,
    proj_recv,
):
    seq_count, group_count, tp_count, per_group, root_scale = dims
    sources = seq_count * group_count
    seq_index = lax.axis_index("seq")
    group_index = lax.axis_index("grp")
    tp_index = lax.axis_index("tp")
    me = seq_index * group_count + group_index
    planes, _, capacity, block_size, head_size = send.shape
    pool_slots = raw[0].shape[0]
    key_heads = planes // 2
    query_rows = all_queries.shape[2]
    groups = query_rows // per_group
    batch_rows, table_width = table_ref.shape
    share_blocks = table_width // seq_count
    positions = per_group * share_blocks
    row_share = parts.shape[2]
    per_tile = groups // row_share
    f32, bf16 = jnp.float32, jnp.bfloat16

    def pool_load(plane):
        return pltpu.make_async_copy(pool_ref.at[:, plane], raw[plane], load_sems.at[plane])

    small_loads = [
        pltpu.make_async_copy(source, target, word_sems.at[4 + place])
        for place, (source, target) in enumerate(
            (
                (table_in, table_ref),
                (lengths_in, lengths_ref),
                (block_scale_in, block_scale_ref),
            )
        )
    ] + [
        pltpu.make_async_copy(
            queries_in.at[request, pl.ds(head * groups, groups)],
            queries_ref.at[head, pl.ds(request * groups, groups)],
            word_sems.at[7 + head * per_group + request],
        )
        for head in range(key_heads)
        for request in range(per_group)
    ]
    for copy in small_loads:
        copy.start()
    pool_load(0).start()

    def source_device(other):
        return {"seq": other // group_count, "grp": other % group_count}

    barrier = pltpu.get_barrier_semaphore()
    for step in range(1, sources):
        pl.semaphore_signal(
            barrier, inc=1, device_id=source_device(xor_index(me, step)), device_id_type=MESH
        )
    for step in range(1, tp_count):
        pl.semaphore_signal(
            barrier,
            inc=1,
            device_id={"tp": xor_index(tp_index, step)},
            device_id_type=MESH,
        )
    for plane in range(1, planes):
        pool_load(plane).start()

    wide = (batch_rows, table_width)
    for copy in small_loads:
        copy.wait()
    table = table_ref[...]
    row_of = lax.broadcasted_iota(jnp.int32, wide, 0)
    col_of = lax.broadcasted_iota(jnp.int32, wide, 1)
    square = (table_width, table_width)
    upper = lax.broadcasted_iota(jnp.int32, square, 0)
    lower = lax.broadcasted_iota(jnp.int32, square, 1)
    alike = upper // share_blocks == lower // share_blocks
    all_alike = jnp.where(alike, 1.0, 0.0).astype(bf16)
    earlier = jnp.where(alike, jnp.where(upper < lower, 1.0, 0.0), 0.0).astype(bf16)
    owner = table // pool_slots
    local = (table % pool_slots).astype(f32)

    def ranks(theirs):
        ones = jnp.where(theirs, 1.0, 0.0).astype(bf16)
        rank = jnp.dot(ones, earlier, preferred_element_type=f32)
        whole = jnp.dot(ones, all_alike, preferred_element_type=f32)
        for request in range(batch_rows):
            last = request // per_group * per_group + per_group
            for later in range(request + 1, last):
                rank = rank + jnp.where(row_of == later, whole[request : request + 1], 0.0)
        return rank

    range_of = jnp.where(upper // share_blocks == lower, 1.0, 0.0).astype(bf16)
    own_rank = jnp.where(owner == me, ranks(owner == me), -1.0)

    def pick(kind, values):
        for within in range(capacity):
            pick_rows[kind, within] = jnp.dot(
                jnp.where(own_rank == within, values, 0.0).astype(bf16),
                range_of,
                preferred_element_type=f32,
            ).astype(jnp.int32)
        return pltpu.make_async_copy(
            pick_rows.at[kind], pick_words.at[kind], word_sems.at[kind]
        )

    slot_copy = pick(0, local)
    slot_copy.start()
    own_queries = pltpu.make_async_copy(queries_ref, all_queries.at[group_index], local_sems.at[0])
    own_queries.start()
    pl.semaphore_wait(barrier, sources - 1 + tp_count - 1)

    def query_copy(step):
        return pltpu.make_async_remote_copy(
            src_ref=queries_ref,
            dst_ref=all_queries.at[group_index],
            send_sem=query_send.at[step],
            recv_sem=query_recv.at[step],
            device_id={"grp": xor_index(group_index, step)},
            device_id_type=MESH,
        )

    for step in range(1, group_count):
        query_copy(step).start()

    def scale_copy(step):
        return pltpu.make_async_remote_copy(
            src_ref=block_scale_ref,
            dst_ref=scales_in.at[me],
            send_sem=scale_send.at[step],
            recv_sem=scale_recv.at[step],
            device_id=source_device(xor_index(me, step)),
            device_id_type=MESH,
        )

    own_scales = pltpu.make_async_copy(block_scale_ref, scales_in.at[me], local_sems.at[1])

    def block_copy(plane, step):
        other = xor_index(me, step)
        return pltpu.make_async_remote_copy(
            src_ref=send.at[plane, other],
            dst_ref=arrived[plane].at[pl.ds(me * capacity, capacity)],
            send_sem=block_send.at[plane, step],
            recv_sem=block_recv.at[plane, step],
            device_id=source_device(other),
            device_id_type=MESH,
        )

    def own_blocks(plane):
        return pltpu.make_async_copy(
            send.at[plane, me],
            arrived[plane].at[pl.ds(me * capacity, capacity)],
            local_sems.at[2 + plane],
        )

    steps = sorted(range(1, sources), key=lambda s: (s // group_count == 0, s % group_count, s))

    def picked(kind, other, within, request):
        group = other % group_count
        return pick_words[kind, within, group * per_group + request, other // group_count]

    def slot_of(other, within):
        slot = picked(0, other, within, 0)
        for request in range(1, per_group):
            slot = slot + picked(0, other, within, request)
        return jnp.clip(slot, 0, pool_slots - 1)

    def sort_blocks(plane, other):
        def place(within, _):
            send[plane, other, within] = raw[plane][slot_of(other, within)]
            return 0

        lax.fori_loop(0, capacity, place, 0)

    def sort_plane(plane):
        def place(other, _):
            sort_blocks(plane, other)
            return 0

        lax.fori_loop(0, sources, place, 0)

    def send_plane(plane):
        for step in steps:
            block_copy(plane, step).start()
        own_blocks(plane).start()

    slot_copy.wait()
    pool_load(0).wait()
    for place, step in enumerate(steps):
        sort_blocks(0, xor_index(me, step))
        if place:
            block_copy(0, steps[place - 1]).start()
    sort_blocks(0, me)
    block_copy(0, steps[-1]).start()
    for step in steps:
        scale_copy(step).start()
    own_scales.start()
    weight_load = pltpu.make_async_copy(weight_ref, weights, load_sems.at[planes])
    weight_load.start()
    for plane in range(1, planes):
        pool_load(plane).wait()
        sort_plane(plane)
    own_blocks(0).start()

    arrival = jnp.zeros(wide, f32)
    for source in range(sources):
        theirs = owner == source
        arrival = jnp.where(theirs, ranks(theirs) + source * capacity, arrival)
    arrival_rows[...] = arrival.astype(jnp.int32)
    context = jnp.full(wide, lengths_ref[0], jnp.int32)
    for request in range(1, batch_rows):
        context = jnp.where(row_of == request, lengths_ref[request], context)
    live = jnp.clip(context - col_of * block_size, 0, block_size).astype(f32)
    scales_wide[...] = block_scale_ref[...].astype(f32)
    word_copies = [
        pick(1, live),
        pltpu.make_async_copy(arrival_rows, arrival_words, word_sems.at[2]),
        pltpu.make_async_copy(scales_wide, scale_words, word_sems.at[3]),
    ]
    for copy in word_copies:
        copy.start()
    for copy in word_copies:
        copy.wait()

    own_queries.wait()
    for step in range(1, group_count):
        query_copy(step).wait()

    lanes = lax.broadcasted_iota(jnp.int32, (query_rows, block_size), 1)
    row_ids = lax.broadcasted_iota(jnp.int32, (query_rows, block_size), 0)
    for head in range(key_heads):
        peaks[...] = jnp.full_like(peaks, absent_score)
        sums[...] = jnp.zeros_like(sums)
        accums[...] = jnp.zeros_like(accums)

        def score_blocks(other, _):
            group = other % group_count
            keys = send[2 * head, other].reshape(capacity * block_size, head_size)
            raw_scores = lax.dot_general(
                all_queries[group, head],
                keys,
                (((1,), (1,)), ((), ())),
                preferred_element_type=jnp.float32,
            )
            highest = peaks[group]
            for within in range(capacity):
                limit = jnp.full(lanes.shape, picked(1, other, within, 0), jnp.int32)
                for request in range(1, per_group):
                    limit = jnp.where(
                        row_ids >= request * groups, picked(1, other, within, request), limit
                    )
                part = raw_scores[:, within * block_size : (within + 1) * block_size]
                part = part * scale_words[2 * head, slot_of(other, within)] * root_scale
                part = jnp.where(lanes < limit, part, absent_score)
                scores[other, :, within * block_size : (within + 1) * block_size] = part
                highest = jnp.maximum(highest, part)
            peaks[group] = highest
            return 0

        lax.fori_loop(0, sources, score_blocks, 0)
        for group in range(group_count):
            peaks[group] = jnp.broadcast_to(
                jnp.max(peaks[group], axis=1, keepdims=True), lanes.shape
            )

        def weigh_blocks(other, _):
            group = other % group_count
            peak = peaks[group]
            total = sums[group]
            pieces = []
            for within in range(capacity):
                part = scores[other, :, within * block_size : (within + 1) * block_size]
                weight = jnp.where(part > absent_limit, jnp.exp(part - peak), 0.0)
                total = total + weight
                pieces.append(
                    (weight * scale_words[2 * head + 1, slot_of(other, within)]).astype(bf16)
                )
            sums[group] = total
            values = send[2 * head + 1, other].reshape(capacity * block_size, head_size)
            accums[group] += jnp.dot(
                jnp.concatenate(pieces, axis=1), values, preferred_element_type=jnp.float32
            )
            return 0

        lax.fori_loop(0, sources, weigh_blocks, 0)
        for group in range(group_count):
            total = jnp.broadcast_to(jnp.sum(sums[group], axis=1, keepdims=True), lanes.shape)
            for request in range(per_group):
                tile = (group * key_heads + head) * per_group + request
                for piece in range(per_tile):
                    low = request * groups + piece * row_share
                    place = tile * per_tile + piece
                    parts[place, 0] = accums[group, low : low + row_share]
                    parts[place, 1] = peaks[group, low : low + row_share]
                    parts[place, 2] = total[low : low + row_share]

    def part_copy(step):
        other = xor_index(me, step)
        return pltpu.make_async_remote_copy(
            src_ref=parts.at[other],
            dst_ref=parts_in.at[me],
            send_sem=part_send.at[step],
            recv_sem=part_recv.at[step],
            device_id=source_device(other),
            device_id_type=MESH,
        )

    for step in steps:
        part_copy(step).start()
    own_part = pltpu.make_async_copy(parts.at[me], parts_in.at[me], local_sems.at[2 + planes])
    own_part.start()
    if planes > 1:
        send_plane(1)
    own_part.wait()
    for step in steps:
        part_copy(step).wait_recv()

    highest = parts_in[0, 1]
    for source in range(1, sources):
        highest = jnp.maximum(highest, parts_in[source, 1])
    numerator = jnp.zeros_like(highest)
    denominator = jnp.zeros_like(highest)
    for source in range(sources):
        factor = jnp.exp(parts_in[source, 1] - highest)
        numerator += parts_in[source, 0] * factor
        denominator += parts_in[source, 2] * factor
    attended[me] = (numerator / denominator).astype(jnp.bfloat16).astype(jnp.float32)

    def att_copy(step):
        return pltpu.make_async_remote_copy(
            src_ref=attended.at[me],
            dst_ref=attended.at[me],
            send_sem=att_send.at[step],
            recv_sem=att_recv.at[step],
            device_id=source_device(xor_index(me, step)),
            device_id_type=MESH,
        )

    weight_load.wait()
    for step in steps:
        att_copy(step).start()
    for plane in range(2, planes):
        send_plane(plane)
    for step in steps:
        att_copy(step).wait_recv()

    rows = sources * row_share
    gathered = attended[...].reshape(rows, head_size)
    row = lax.broadcasted_iota(jnp.int32, (rows, head_size), 0)
    row_head = (row // (groups * per_group)) % key_heads * groups + row % groups
    left = jnp.concatenate(
        [
            jnp.where(row_head == head, gathered, 0.0).astype(jnp.bfloat16)
            for head in range(key_heads * groups)
        ],
        axis=1,
    )
    columns = weights.shape[1]
    width = min(columns, 256)
    here = batch_rows // tp_count
    for low in range(0, columns, width):
        product = jnp.dot(left, weights[:, low : low + width], preferred_element_type=jnp.float32)
        for request in range(batch_rows):
            group, inner = request // per_group, request % per_group
            total = jnp.zeros((1, width), jnp.float32)
            for head in range(key_heads):
                tile = (group * key_heads + head) * per_group + inner
                total += jnp.sum(
                    product[tile * groups : (tile + 1) * groups], axis=0, keepdims=True
                )
            projected[request // here, pl.ds(request % here, 1), low : low + width] = total

    def proj_copy(step):
        other = xor_index(tp_index, step)
        return pltpu.make_async_remote_copy(
            src_ref=projected.at[other],
            dst_ref=projected_in.at[tp_index],
            send_sem=proj_send.at[step],
            recv_sem=proj_recv.at[step],
            device_id={"tp": other},
            device_id_type=MESH,
        )

    for step in range(1, tp_count):
        proj_copy(step).start()
    projected_in[tp_index] = projected[tp_index]
    for step in range(1, tp_count):
        proj_copy(step).wait()
    total = projected_in[0]
    for source in range(1, tp_count):
        total += projected_in[source]
    output_ref[...] = total.astype(output_ref.dtype)

    own_scales.wait()
    for step in steps:
        scale_copy(step).wait()
    slot_ids = lax.broadcasted_iota(jnp.int32, (pool_slots, table_width), 0)
    wanted = jnp.where(
        lax.broadcasted_iota(jnp.int32, (table_width, share_blocks), 0)
        == lax.broadcasted_iota(jnp.int32, (table_width, share_blocks), 1)
        + seq_index * share_blocks,
        1.0,
        0.0,
    ).astype(bf16)
    for request in range(per_group):
        slots = table_ref[pl.ds(group_index * per_group + request, 1), :]
        found = jnp.zeros((planes, table_width), f32)
        for source in range(sources):
            onehot = jnp.where(slots == slot_ids + source * pool_slots, 1.0, 0.0).astype(bf16)
            found += jnp.dot(scales_in[source], onehot, preferred_element_type=f32)
        scales_out_ref[request] = jnp.dot(
            found.astype(bf16), wanted, preferred_element_type=f32
        ).astype(bf16)

    unroll = 4 if share_blocks % 4 == 0 else 1
    for plane in range(planes):
        own_blocks(plane).wait()
        for step in steps:
            block_copy(plane, step).wait_recv()
        for request in range(per_group):

            def place(turn, _):
                for part in range(unroll):
                    column = turn * unroll + part
                    index = arrival_words[
                        group_index * per_group + request, seq_index * share_blocks + column
                    ]
                    placed_ref[request * share_blocks + column, plane] = arrived[plane][
                        jnp.clip(index, 0, positions - 1)
                    ]
                return 0

            lax.fori_loop(0, share_blocks // unroll, place, 0)
    for step in steps:
        part_copy(step).wait_send()
        att_copy(step).wait_send()
        for plane in range(planes):
            block_copy(plane, step).wait_send()


def copy_out_kernel(cache_in, scale_in, output_in, cache_ref, scale_ref, output_ref, sems):
    share = cache_in.shape[0] // 4
    copies = [
        pltpu.make_async_copy(
            cache_in.at[pl.ds(part * share, share)],
            cache_ref.at[pl.ds(part * share, share)],
            sems.at[part],
        )
        for part in range(4)
    ]
    copies.append(pltpu.make_async_copy(scale_in, scale_ref, sems.at[4]))
    copies.append(pltpu.make_async_copy(output_in, output_ref, sems.at[5]))
    for copy in copies:
        copy.start()
    for copy in copies:
        copy.wait()


def per_device(queries, cache_pool, block_scale, block_table, lengths, output_weight):
    seq_count = lax.axis_size("seq")
    group_count = lax.axis_size("grp")
    tp_count = lax.axis_size("tp")
    sources = seq_count * group_count
    pool_slots, key_heads, _, block_size, head_size = cache_pool.shape
    batch_rows, table_width = block_table.shape
    per_group = batch_rows // group_count
    share_blocks = table_width // seq_count
    capacity = pool_slots // sources
    heads_here = queries.shape[1]
    groups = heads_here // key_heads
    planes = key_heads * 2
    positions = per_group * share_blocks
    columns = output_weight.shape[1]
    root_scale = 1.0 / math.sqrt(head_size)

    row_share = batch_rows * key_heads * groups // sources
    query_rows = per_group * groups
    f32, bf16 = jnp.float32, jnp.bfloat16
    dma = pltpu.SemaphoreType.DMA
    vmem = pl.BlockSpec(memory_space=pltpu.VMEM)
    hbm = pl.BlockSpec(memory_space=pltpu.HBM)
    here = batch_rows // tp_count
    decode_cache, decode_scale, output = pl.pallas_call(
        functools.partial(
            exchange_kernel, (seq_count, group_count, tp_count, per_group, root_scale)
        ),
        out_shape=(
            pltpu.VMEM((positions, planes, block_size, head_size), bf16),
            pltpu.VMEM((per_group, planes, share_blocks), bf16),
            pltpu.VMEM((here, columns), bf16),
        ),
        in_specs=[hbm, hbm, hbm, hbm, hbm, hbm],
        out_specs=(vmem, vmem, vmem),
        scratch_shapes=[
            pltpu.SMEM((batch_rows,), jnp.int32),
            pltpu.VMEM((batch_rows, table_width), jnp.int32),
            pltpu.VMEM((planes, pool_slots), bf16),
            pltpu.VMEM((key_heads, query_rows, head_size), bf16),
            [pltpu.VMEM((pool_slots, block_size, head_size), bf16) for _ in range(planes)],
            pltpu.VMEM((planes, sources, capacity, block_size, head_size), bf16),
            [pltpu.VMEM((pool_slots, block_size, head_size), bf16) for _ in range(planes)],
            pltpu.VMEM((heads_here * head_size, columns), bf16),
            pltpu.VMEM((group_count, key_heads, query_rows, head_size), bf16),
            pltpu.VMEM((sources, query_rows, capacity * block_size), f32),
            pltpu.VMEM((group_count, query_rows, block_size), f32),
            pltpu.VMEM((group_count, query_rows, block_size), f32),
            pltpu.VMEM((group_count, query_rows, head_size), f32),
            pltpu.VMEM((sources, 3, row_share, head_size), f32),
            pltpu.VMEM((sources, 3, row_share, head_size), f32),
            pltpu.VMEM((sources, row_share, head_size), f32),
            pltpu.VMEM((tp_count, here, columns), f32),
            pltpu.VMEM((tp_count, here, columns), f32),
            pltpu.VMEM((sources, planes, pool_slots), bf16),
            pltpu.VMEM((planes, pool_slots), f32),
            pltpu.VMEM((batch_rows, table_width), jnp.int32),
            pltpu.VMEM((2, capacity, batch_rows, table_width), jnp.int32),
            pltpu.SMEM((planes, pool_slots), f32),
            pltpu.SMEM((batch_rows, table_width), jnp.int32),
            pltpu.SMEM((2, capacity, batch_rows, table_width), jnp.int32),
            dma((planes + 1,)),
            dma((planes + 3,)),
            dma((7 + key_heads * per_group,)),
            dma((planes, sources)),
            dma((planes, sources)),
            dma((group_count,)),
            dma((group_count,)),
            dma((sources,)),
            dma((sources,)),
            dma((sources,)),
            dma((sources,)),
            dma((sources,)),
            dma((sources,)),
            dma((tp_count,)),
            dma((tp_count,)),
        ],
        compiler_params=pltpu.CompilerParams(
            collective_id=0, has_side_effects=True, vmem_limit_bytes=40 * 2**20
        ),
    )(
        *(
            pltpu.with_memory_space_constraint(operand, pltpu.HBM)
            for operand in (
                lengths,
                block_table,
                block_scale.reshape(pool_slots, planes).T,
                queries,
                cache_pool.reshape(pool_slots, planes, block_size, head_size),
                output_weight,
            )
        )
    )
    results = (decode_cache, decode_scale, output)
    decode_cache, decode_scale, output = pl.pallas_call(
        copy_out_kernel,
        out_shape=tuple(jax.ShapeDtypeStruct(r.shape, r.dtype) for r in results),
        in_specs=[vmem] * 3,
        out_specs=(hbm,) * 3,
        scratch_shapes=[dma((6,))],
        compiler_params=pltpu.CompilerParams(vmem_limit_bytes=16 * 2**20),
    )(*(pltpu.with_memory_space_constraint(r, pltpu.VMEM) for r in results))
    return (
        output,
        decode_cache.reshape(per_group, share_blocks, key_heads, 2, block_size, head_size),
        decode_scale.transpose(0, 2, 1).reshape(per_group, share_blocks, key_heads, 2),
    )


def solution(mesh):
    placed = (
        P("grp", "tp", None),
        P(("seq", "grp"), "tp", None, None, None),
        P(("seq", "grp"), "tp", None),
        P(),
        P(),
        P("tp", ("seq", "grp")),
    )
    return jax.shard_map(
        per_device,
        mesh=mesh,
        in_specs=placed,
        out_specs=(
            P("tp", ("seq", "grp")),
            P("grp", "seq", "tp", None, None, None),
            P("grp", "seq", "tp", None),
        ),
        check_vma=False,
    )
```

profile of v0, /device:TPU:1, one launch (start us, length us, event | category | flops | bytes accessed | tf_op | source)
XLA Modules:
  0.0 105.1 jit_solution(9667296370329707053)
XLA Ops:
  0.6 101.1 %shard_map.85 = (bf16[64,4,128,128]{3,2,1,0:T(8,128)(2,1)S(1)}, bf16[2,4,32]{2,1,0:T(4,128)(2,1)S(1)}, bf16[1,1024]{1,0:T(2,128)(2,1)S(1)}) custom-call(s32[4]{0:T(128)} %lengths_in.1, s32[4,128]{1,0:T(4,128)} %table_in.1, bf16[4,64]{1,0:T(4,128)(2,1)} %bitcast.9, bf16[2,16,128]{2,1,0:T(8,128)(2,1)} %queries_in.1, bf16[64,4,128,128]{3,2,1,0:T(8,128)(2,1)} %bitcast.8, ...), custom_call_target="tpu_custom_call" | custom-call | tf_op jit(solution)/shard_map/pallas_call | solution.py:554
  101.7 3.4 %shard_map.86 = (bf16[64,4,128,128]{3,2,1,0:T(8,128)(2,1)}, bf16[2,4,32]{2,1,0:T(4,128)(2,1)}, bf16[1,1024]{1,0:T(2,128)(2,1)}) custom-call(bf16[64,4,128,128]{3,2,1,0:T(8,128)(2,1)S(1)} %get-tuple-element.9.cache_in, bf16[2,4,32]{2,1,0:T(4,128)(2,1)S(1)} %get-tuple-element.10.scale_in, bf16[1,1024]{1,0:T(2,128)(2,1)S(1)} %get-tuple-element.11.output_in), custom_call_target="tpu_custom_call" | custom-call | tf_op jit(solution)/shard_map/pallas_call | solution.py:624
where the time goes:
time: 105 us
  Pallas kernels  104 us (99%)
    pallas_call x1, Pallas kernels, per_device(): pl.pallas_call(functools.partial(exchange_kernel, (seq_count, group_count...  101 us
    pallas_call x1, Pallas kernels, per_device(): pl.pallas_call(copy_out_kernel, out_shape=tuple((jax.ShapeDtypeStruct(r.s...  3.39 us

commit v1 on v0

--- a/solution.py
+++ b/solution.py
@@ -49,6 +49,8 @@
     accums,
     parts,
     parts_in,
+    stats,
+    stats_in,
     attended,
     projected,
     projected_in,
@@ -70,6 +72,10 @@
     scale_recv,
     part_send,
     part_recv,
+    stat_send,
+    stat_recv,
+    known_below,
+    known_above,
     att_send,
     att_recv,
     proj_send,
@@ -89,22 +95,17 @@
     batch_rows, table_width = table_ref.shape
     share_blocks = table_width // seq_count
     positions = per_group * share_blocks
-    row_share = parts.shape[2]
+    row_share = parts.shape[1]
     per_tile = groups // row_share
     f32, bf16 = jnp.float32, jnp.bfloat16
 
     def pool_load(plane):
         return pltpu.make_async_copy(pool_ref.at[:, plane], raw[plane], load_sems.at[plane])
 
+    table_load = pltpu.make_async_copy(table_in, table_ref, word_sems.at[4])
     small_loads = [
-        pltpu.make_async_copy(source, target, word_sems.at[4 + place])
-        for place, (source, target) in enumerate(
-            (
-                (table_in, table_ref),
-                (lengths_in, lengths_ref),
-                (block_scale_in, block_scale_ref),
-            )
-        )
+        pltpu.make_async_copy(lengths_in, lengths_ref, word_sems.at[5]),
+        pltpu.make_async_copy(block_scale_in, block_scale_ref, word_sems.at[6]),
     ] + [
         pltpu.make_async_copy(
             queries_in.at[request, pl.ds(head * groups, groups)],
@@ -114,8 +115,7 @@
         for head in range(key_heads)
         for request in range(per_group)
     ]
-    for copy in small_loads:
-        copy.start()
+    table_load.start()
     pool_load(0).start()
 
     def source_device(other):
@@ -126,19 +126,22 @@
         pl.semaphore_signal(
             barrier, inc=1, device_id=source_device(xor_index(me, step)), device_id_type=MESH
         )
-    for step in range(1, tp_count):
+    below, above = tp_index > 0, tp_index < tp_count - 1
+
+    @pl.when(below)
+    def _():
         pl.semaphore_signal(
-            barrier,
-            inc=1,
-            device_id={"tp": xor_index(tp_index, step)},
-            device_id_type=MESH,
-        )
-    for plane in range(1, planes):
-        pool_load(plane).start()
+            barrier, inc=1, device_id={"tp": tp_index - 1}, device_id_type=MESH
+        )
+
+    @pl.when(above)
+    def _():
+        pl.semaphore_signal(
+            barrier, inc=1, device_id={"tp": tp_index + 1}, device_id_type=MESH
+        )
 
     wide = (batch_rows, table_width)
-    for copy in small_loads:
-        copy.wait()
+    table_load.wait()
     table = table_ref[...]
     row_of = lax.broadcasted_iota(jnp.int32, wide, 0)
     col_of = lax.broadcasted_iota(jnp.int32, wide, 1)
@@ -178,8 +181,8 @@
     slot_copy = pick(0, local)
     slot_copy.start()
     own_queries = pltpu.make_async_copy(queries_ref, all_queries.at[group_index], local_sems.at[0])
-    own_queries.start()
-    pl.semaphore_wait(barrier, sources - 1 + tp_count - 1)
+    beside = jnp.where(below, 1, 0) + jnp.where(above, 1, 0)
+    pl.semaphore_wait(barrier, sources - 1 + beside)
 
     def query_copy(step):
         return pltpu.make_async_remote_copy(
@@ -190,9 +193,6 @@
             device_id={"grp": xor_index(group_index, step)},
             device_id_type=MESH,
         )
-
-    for step in range(1, group_count):
-        query_copy(step).start()
 
     def scale_copy(step):
         return pltpu.make_async_remote_copy(
@@ -263,6 +263,15 @@
             block_copy(0, steps[place - 1]).start()
     sort_blocks(0, me)
     block_copy(0, steps[-1]).start()
+    for copy in small_loads:
+        copy.start()
+    for plane in range(1, planes):
+        pool_load(plane).start()
+    for copy in small_loads:
+        copy.wait()
+    own_queries.start()
+    for step in range(1, group_count):
+        query_copy(step).start()
     for step in steps:
         scale_copy(step).start()
     own_scales.start()
@@ -299,6 +308,8 @@
 
     lanes = lax.broadcasted_iota(jnp.int32, (query_rows, block_size), 1)
     row_ids = lax.broadcasted_iota(jnp.int32, (query_rows, block_size), 0)
+    share_lanes = lax.broadcasted_iota(jnp.int32, (row_share, head_size), 1)
+    share_rows = lax.broadcasted_iota(jnp.int32, (row_share, head_size), 0)
     for head in range(key_heads):
         peaks[...] = jnp.full_like(peaks, absent_score)
         sums[...] = jnp.zeros_like(sums)
@@ -361,9 +372,19 @@
                 for piece in range(per_tile):
                     low = request * groups + piece * row_share
                     place = tile * per_tile + piece
-                    parts[place, 0] = accums[group, low : low + row_share]
-                    parts[place, 1] = peaks[group, low : low + row_share]
-                    parts[place, 2] = total[low : low + row_share]
+                    parts[place] = accums[group, low : low + row_share]
+                    stats[place] = jnp.sum(
+                        jnp.where(
+                            share_lanes == share_rows, peaks[group, low : low + row_share], 0.0
+                        )
+                        + jnp.where(
+                            share_lanes == share_rows + row_share,
+                            total[low : low + row_share],
+                            0.0,
+                        ),
+                        axis=0,
+                        keepdims=True,
+                    )
 
     def part_copy(step):
         other = xor_index(me, step)
@@ -376,26 +397,74 @@
             device_id_type=MESH,
         )
 
+    def stat_copy(step):
+        other = xor_index(me, step)
+        return pltpu.make_async_remote_copy(
+            src_ref=stats.at[other],
+            dst_ref=stats_in.at[me],
+            send_sem=stat_send.at[step],
+            recv_sem=stat_recv.at[step],
+            device_id=source_device(other),
+            device_id_type=MESH,
+        )
+
     for step in steps:
+        stat_copy(step).start()
         part_copy(step).start()
-    own_part = pltpu.make_async_copy(parts.at[me], parts_in.at[me], local_sems.at[2 + planes])
-    own_part.start()
+    parts_in[me] = parts[me]
+    stats_in[me] = stats[me]
     if planes > 1:
         send_plane(1)
-    own_part.wait()
+
+    for reach in range(1, tp_count - 1):
+
+        @pl.when(jnp.logical_and(tp_index >= reach, above))
+        def _():
+            pl.semaphore_signal(
+                known_below.at[reach], inc=1, device_id={"tp": tp_index + 1}, device_id_type=MESH
+            )
+
+        @pl.when(jnp.logical_and(tp_index + reach < tp_count, below))
+        def _():
+            pl.semaphore_signal(
+                known_above.at[reach], inc=1, device_id={"tp": tp_index - 1}, device_id_type=MESH
+            )
+
+        @pl.when(tp_index - 1 >= reach)
+        def _():
+            pl.semaphore_wait(known_below.at[reach], 1)
+
+        @pl.when(tp_index + 1 + reach < tp_count)
+        def _():
+            pl.semaphore_wait(known_above.at[reach], 1)
+
     for step in steps:
+        stat_copy(step).wait_recv()
         part_copy(step).wait_recv()
 
-    highest = parts_in[0, 1]
-    for source in range(1, sources):
-        highest = jnp.maximum(highest, parts_in[source, 1])
+    def spread(source, first):
+        return jnp.broadcast_to(
+            jnp.sum(
+                jnp.where(
+                    share_lanes == share_rows + first,
+                    jnp.broadcast_to(stats_in[source], share_lanes.shape),
+                    0.0,
+                ),
+                axis=1,
+                keepdims=True,
+            ),
+            share_lanes.shape,
+        )
+
+    source_peaks = [spread(source, 0) for source in range(sources)]
+    highest = functools.reduce(jnp.maximum, source_peaks)
     numerator = jnp.zeros_like(highest)
     denominator = jnp.zeros_like(highest)
     for source in range(sources):
-        factor = jnp.exp(parts_in[source, 1] - highest)
-        numerator += parts_in[source, 0] * factor
-        denominator += parts_in[source, 2] * factor
-    attended[me] = (numerator / denominator).astype(jnp.bfloat16).astype(jnp.float32)
+        factor = jnp.exp(source_peaks[source] - highest)
+        numerator += parts_in[source] * factor
+        denominator += spread(source, row_share) * factor
+    attended[me] = (numerator / denominator).astype(jnp.bfloat16)
 
     def att_copy(step):
         return pltpu.make_async_remote_copy(
@@ -416,7 +485,7 @@
         att_copy(step).wait_recv()
 
     rows = sources * row_share
-    gathered = attended[...].reshape(rows, head_size)
+    gathered = attended[...].astype(f32).reshape(rows, head_size)
     row = lax.broadcasted_iota(jnp.int32, (rows, head_size), 0)
     row_head = (row // (groups * per_group)) % key_heads * groups + row % groups
     left = jnp.concatenate(
@@ -504,6 +573,7 @@
             lax.fori_loop(0, share_blocks // unroll, place, 0)
     for step in steps:
         part_copy(step).wait_send()
+        stat_copy(step).wait_send()
         att_copy(step).wait_send()
         for plane in range(planes):
             block_copy(plane, step).wait_send()
@@ -576,9 +646,11 @@
             pltpu.VMEM((group_count, query_rows, block_size), f32),
             pltpu.VMEM((group_count, query_rows, block_size), f32),
             pltpu.VMEM((group_count, query_rows, head_size), f32),
-            pltpu.VMEM((sources, 3, row_share, head_size), f32),
-            pltpu.VMEM((sources, 3, row_share, head_size), f32),
             pltpu.VMEM((sources, row_share, head_size), f32),
+            pltpu.VMEM((sources, row_share, head_size), f32),
+            pltpu.VMEM((sources, 1, head_size), f32),
+            pltpu.VMEM((sources, 1, head_size), f32),
+            pltpu.VMEM((sources, row_share, head_size), bf16),
             pltpu.VMEM((tp_count, here, columns), f32),
             pltpu.VMEM((tp_count, here, columns), f32),
             pltpu.VMEM((sources, planes, pool_slots), bf16),
@@ -601,6 +673,10 @@
             dma((sources,)),
             dma((sources,)),
             dma((sources,)),
+            pltpu.SemaphoreType.REGULAR((tp_count,)),
+            pltpu.SemaphoreType.REGULAR((tp_count,)),
+            dma((sources,)),
+            dma((sources,)),
             dma((tp_count,)),
             dma((tp_count,)),
         ],

time: 105 us -> 103 us (0.981)
  Pallas kernels: 104 us -> 102 us
    pallas_call x1, Pallas kernels: 101 us -> 98.8 us  [per_device(): pl.pallas_call(functools.partial(exchange_kernel, (seq_count, group_count...]
where the time goes in v1:
time: 103 us
  Pallas kernels  102 us (99%)
    pallas_call x1, Pallas kernels, per_device(): pl.pallas_call(functools.partial(exchange_kernel, (seq_count, group_count...  98.8 us
    pallas_call x1, Pallas kernels, per_device(): pl.pallas_call(copy_out_kernel, out_shape=tuple((jax.ShapeDtypeStruct(r.s...  3.39 us

profile of v1, /device:TPU:1, one launch (start us, length us, event | category | flops | bytes accessed | tf_op | source)
XLA Modules:
  0.0 102.8 jit_solution(17628256197922770606)
XLA Ops:
  0.6 98.8 %shard_map.85 = (bf16[64,4,128,128]{3,2,1,0:T(8,128)(2,1)S(1)}, bf16[2,4,32]{2,1,0:T(4,128)(2,1)S(1)}, bf16[1,1024]{1,0:T(2,128)(2,1)S(1)}) custom-call(s32[4]{0:T(128)} %lengths_in.1, s32[4,128]{1,0:T(4,128)} %table_in.1, bf16[4,64]{1,0:T(4,128)(2,1)} %bitcast.9, bf16[2,16,128]{2,1,0:T(8,128)(2,1)} %queries_in.1, bf16[64,4,128,128]{3,2,1,0:T(8,128)(2,1)} %bitcast.8, ...), custom_call_target="tpu_custom_call" | custom-call | tf_op jit(solution)/shard_map/pallas_call | solution.py:624
  99.4 3.4 %shard_map.86 = (bf16[64,4,128,128]{3,2,1,0:T(8,128)(2,1)}, bf16[2,4,32]{2,1,0:T(4,128)(2,1)}, bf16[1,1024]{1,0:T(2,128)(2,1)}) custom-call(bf16[64,4,128,128]{3,2,1,0:T(8,128)(2,1)S(1)} %get-tuple-element.9.cache_in, bf16[2,4,32]{2,1,0:T(4,128)(2,1)S(1)} %get-tuple-element.10.scale_in, bf16[1,1024]{1,0:T(2,128)(2,1)S(1)} %get-tuple-element.11.output_in), custom_call_target="tpu_custom_call" | custom-call | tf_op jit(solution)/shard_map/pallas_call | solution.py:700

commit v2 on v1

--- a/solution.py
+++ b/solution.py
@@ -32,6 +32,8 @@
     pool_ref,
     weight_ref,
     placed_ref,
+    last_ref,
+    arrival_rows,
     scales_out_ref,
     output_ref,
     lengths_ref,
@@ -56,7 +58,6 @@
     projected_in,
     scales_in,
     scales_wide,
-    arrival_rows,
     pick_rows,
     scale_words,
     arrival_words,
@@ -88,6 +89,7 @@
     tp_index = lax.axis_index("tp")
     me = seq_index * group_count + group_index
     planes, _, capacity, block_size, head_size = send.shape
+    arrived = [*arrived, last_ref]
     pool_slots = raw[0].shape[0]
     key_heads = planes // 2
     query_rows = all_queries.shape[2]
@@ -127,12 +129,6 @@
             barrier, inc=1, device_id=source_device(xor_index(me, step)), device_id_type=MESH
         )
     below, above = tp_index > 0, tp_index < tp_count - 1
-
-    @pl.when(below)
-    def _():
-        pl.semaphore_signal(
-            barrier, inc=1, device_id={"tp": tp_index - 1}, device_id_type=MESH
-        )
 
     @pl.when(above)
     def _():
@@ -181,8 +177,7 @@
     slot_copy = pick(0, local)
     slot_copy.start()
     own_queries = pltpu.make_async_copy(queries_ref, all_queries.at[group_index], local_sems.at[0])
-    beside = jnp.where(below, 1, 0) + jnp.where(above, 1, 0)
-    pl.semaphore_wait(barrier, sources - 1 + beside)
+    pl.semaphore_wait(barrier, sources - 1 + jnp.where(below, 1, 0))
 
     def query_copy(step):
         return pltpu.make_async_remote_copy(
@@ -225,6 +220,8 @@
         )
 
     steps = sorted(range(1, sources), key=lambda s: (s // group_count == 0, s % group_count, s))
+    near_steps = [s for s in steps if (s // group_count).bit_count() <= 1]
+    far_steps = [s for s in steps if s not in near_steps]
 
     def picked(kind, other, within, request):
         group = other % group_count
@@ -250,19 +247,20 @@
 
         lax.fori_loop(0, sources, place, 0)
 
-    def send_plane(plane):
-        for step in steps:
+    def send_plane(plane, chosen):
+        for step in chosen:
             block_copy(plane, step).start()
-        own_blocks(plane).start()
 
     slot_copy.wait()
     pool_load(0).wait()
-    for place, step in enumerate(steps):
-        sort_blocks(0, xor_index(me, step))
+    for place, step in enumerate(near_steps):
+        other = xor_index(me, step)
+        for within in range(capacity):
+            send[0, other, within] = raw[0][slot_of(other, within)]
         if place:
-            block_copy(0, steps[place - 1]).start()
+            block_copy(0, near_steps[place - 1]).start()
     sort_blocks(0, me)
-    block_copy(0, steps[-1]).start()
+    block_copy(0, near_steps[-1]).start()
     for copy in small_loads:
         copy.start()
     for plane in range(1, planes):
@@ -277,10 +275,15 @@
     own_scales.start()
     weight_load = pltpu.make_async_copy(weight_ref, weights, load_sems.at[planes])
     weight_load.start()
+    for step in far_steps:
+        sort_blocks(0, xor_index(me, step))
     for plane in range(1, planes):
         pool_load(plane).wait()
         sort_plane(plane)
-    own_blocks(0).start()
+        if plane == 1:
+            send_plane(plane, near_steps)
+    for plane in range(planes):
+        own_blocks(plane).start()
 
     arrival = jnp.zeros(wide, f32)
     for source in range(sources):
@@ -372,7 +375,7 @@
                 for piece in range(per_tile):
                     low = request * groups + piece * row_share
                     place = tile * per_tile + piece
-                    parts[place] = accums[group, low : low + row_share]
+                    parts[place] = accums[group, low : low + row_share].astype(bf16)
                     stats[place] = jnp.sum(
                         jnp.where(
                             share_lanes == share_rows, peaks[group, low : low + row_share], 0.0
@@ -413,8 +416,18 @@
         part_copy(step).start()
     parts_in[me] = parts[me]
     stats_in[me] = stats[me]
-    if planes > 1:
-        send_plane(1)
+    for plane in range(2, min(planes, 3)):
+        send_plane(plane, near_steps)
+
+    @pl.when(below)
+    def _():
+        pl.semaphore_signal(
+            known_above.at[0], inc=1, device_id={"tp": tp_index - 1}, device_id_type=MESH
+        )
+
+    @pl.when(above)
+    def _():
+        pl.semaphore_wait(known_above.at[0], 1)
 
     for reach in range(1, tp_count - 1):
 
@@ -462,7 +475,7 @@
     denominator = jnp.zeros_like(highest)
     for source in range(sources):
         factor = jnp.exp(source_peaks[source] - highest)
-        numerator += parts_in[source] * factor
+        numerator += parts_in[source].astype(f32) * factor
         denominator += spread(source, row_share) * factor
     attended[me] = (numerator / denominator).astype(jnp.bfloat16)
 
@@ -479,10 +492,15 @@
     weight_load.wait()
     for step in steps:
         att_copy(step).start()
-    for plane in range(2, planes):
-        send_plane(plane)
+    for plane in range(3, planes):
+        send_plane(plane, near_steps)
     for step in steps:
         att_copy(step).wait_recv()
+    for plane in range(planes):
+        for step in near_steps:
+            block_copy(plane, step).wait_send()
+    for plane in range(planes):
+        send_plane(plane, far_steps)
 
     rows = sources * row_share
     gathered = attended[...].astype(f32).reshape(rows, head_size)
@@ -553,7 +571,7 @@
         ).astype(bf16)
 
     unroll = 4 if share_blocks % 4 == 0 else 1
-    for plane in range(planes):
+    for plane in range(planes - 1):
         own_blocks(plane).wait()
         for step in steps:
             block_copy(plane, step).wait_recv()
@@ -575,26 +593,69 @@
         part_copy(step).wait_send()
         stat_copy(step).wait_send()
         att_copy(step).wait_send()
-        for plane in range(planes):
+    own_blocks(planes - 1).wait()
+    for step in near_steps:
+        block_copy(planes - 1, step).wait_recv()
+    for plane in range(planes):
+        for step in far_steps:
             block_copy(plane, step).wait_send()
-
-
-def copy_out_kernel(cache_in, scale_in, output_in, cache_ref, scale_ref, output_ref, sems):
-    share = cache_in.shape[0] // 4
+    for step in far_steps:
+        block_copy(planes - 1, step).wait_recv()
+
+
+def copy_out_kernel(
+    placed_in,
+    last_in,
+    arrival_in,
+    scale_in,
+    output_in,
+    cache_ref,
+    scale_ref,
+    output_ref,
+    arrival_words,
+    sems,
+    block_sem,
+):
+    positions, first = placed_in.shape[:2]
+    per_group, _, share_blocks = scale_in.shape
+    group_index, seq_index = lax.axis_index("grp"), lax.axis_index("seq")
+    words = pltpu.make_async_copy(arrival_in, arrival_words, sems.at[0])
+    words.start()
+    chunks = 8
+    share = positions // chunks
     copies = [
         pltpu.make_async_copy(
-            cache_in.at[pl.ds(part * share, share)],
-            cache_ref.at[pl.ds(part * share, share)],
-            sems.at[part],
-        )
-        for part in range(4)
+            placed_in.at[pl.ds(part * share, share)],
+            cache_ref.at[pl.ds(part * share, share), pl.ds(0, first)],
+            sems.at[3 + part],
+        )
+        for part in range(chunks)
     ]
-    copies.append(pltpu.make_async_copy(scale_in, scale_ref, sems.at[4]))
-    copies.append(pltpu.make_async_copy(output_in, output_ref, sems.at[5]))
+    copies.append(pltpu.make_async_copy(scale_in, scale_ref, sems.at[1]))
+    copies.append(pltpu.make_async_copy(output_in, output_ref, sems.at[2]))
     for copy in copies:
         copy.start()
+    words.wait()
+
+    def block(position):
+        index = arrival_words[
+            group_index * per_group + position // share_blocks,
+            seq_index * share_blocks + position % share_blocks,
+        ]
+        return pltpu.make_async_copy(
+            last_in.at[jnp.clip(index, 0, positions - 1)],
+            cache_ref.at[position, first],
+            block_sem,
+        )
+
+    def start(position, _):
+        block(position).start()
+        return 0
+
+    lax.fori_loop(0, positions, start, 0, unroll=4)
     for copy in copies:
         copy.wait()
+    pltpu.make_async_copy(last_in, cache_ref.at[:, first], block_sem).wait()
 
 
 def per_device(queries, cache_pool, block_scale, block_table, lengths, output_weight):
@@ -621,17 +682,19 @@
     vmem = pl.BlockSpec(memory_space=pltpu.VMEM)
     hbm = pl.BlockSpec(memory_space=pltpu.HBM)
     here = batch_rows // tp_count
-    decode_cache, decode_scale, output = pl.pallas_call(
+    results = pl.pallas_call(
         functools.partial(
             exchange_kernel, (seq_count, group_count, tp_count, per_group, root_scale)
         ),
         out_shape=(
-            pltpu.VMEM((positions, planes, block_size, head_size), bf16),
+            pltpu.VMEM((positions, planes - 1, block_size, head_size), bf16),
+            pltpu.VMEM((positions, block_size, head_size), bf16),
+            pltpu.VMEM((batch_rows, table_width), jnp.int32),
             pltpu.VMEM((per_group, planes, share_blocks), bf16),
             pltpu.VMEM((here, columns), bf16),
         ),
         in_specs=[hbm, hbm, hbm, hbm, hbm, hbm],
-        out_specs=(vmem, vmem, vmem),
+        out_specs=(vmem,) * 5,
         scratch_shapes=[
             pltpu.SMEM((batch_rows,), jnp.int32),
             pltpu.VMEM((batch_rows, table_width), jnp.int32),
@@ -639,15 +702,15 @@
             pltpu.VMEM((key_heads, query_rows, head_size), bf16),
             [pltpu.VMEM((pool_slots, block_size, head_size), bf16) for _ in range(planes)],
             pltpu.VMEM((planes, sources, capacity, block_size, head_size), bf16),
-            [pltpu.VMEM((pool_slots, block_size, head_size), bf16) for _ in range(planes)],
+            [pltpu.VMEM((pool_slots, block_size, head_size), bf16) for _ in range(planes - 1)],
             pltpu.VMEM((heads_here * head_size, columns), bf16),
             pltpu.VMEM((group_count, key_heads, query_rows, head_size), bf16),
             pltpu.VMEM((sources, query_rows, capacity * block_size), f32),
             pltpu.VMEM((group_count, query_rows, block_size), f32),
             pltpu.VMEM((group_count, query_rows, block_size), f32),
             pltpu.VMEM((group_count, query_rows, head_size), f32),
-            pltpu.VMEM((sources, row_share, head_size), f32),
-            pltpu.VMEM((sources, row_share, head_size), f32),
+            pltpu.VMEM((sources, row_share, head_size), bf16),
+            pltpu.VMEM((sources, row_share, head_size), bf16),
             pltpu.VMEM((sources, 1, head_size), f32),
             pltpu.VMEM((sources, 1, head_size), f32),
             pltpu.VMEM((sources, row_share, head_size), bf16),
@@ -655,7 +718,6 @@
             pltpu.VMEM((tp_count, here, columns), f32),
             pltpu.VMEM((sources, planes, pool_slots), bf16),
             pltpu.VMEM((planes, pool_slots), f32),
-            pltpu.VMEM((batch_rows, table_width), jnp.int32),
             pltpu.VMEM((2, capacity, batch_rows, table_width), jnp.int32),
             pltpu.SMEM((planes, pool_slots), f32),
             pltpu.SMEM((batch_rows, table_width), jnp.int32),
@@ -696,13 +758,20 @@
             )
         )
     )
-    results = (decode_cache, decode_scale, output)
     decode_cache, decode_scale, output = pl.pallas_call(
         copy_out_kernel,
-        out_shape=tuple(jax.ShapeDtypeStruct(r.shape, r.dtype) for r in results),
-        in_specs=[vmem] * 3,
+        out_shape=(
+            jax.ShapeDtypeStruct((positions, planes, block_size, head_size), bf16),
+            jax.ShapeDtypeStruct(results[3].shape, bf16),
+            jax.ShapeDtypeStruct(results[4].shape, bf16),
+        ),
+        in_specs=[vmem] * 5,
         out_specs=(hbm,) * 3,
-        scratch_shapes=[dma((6,))],
+        scratch_shapes=[
+            pltpu.SMEM((batch_rows, table_width), jnp.int32),
+            dma((11,)),
+            dma,
+        ],
         compiler_params=pltpu.CompilerParams(vmem_limit_bytes=16 * 2**20),
     )(*(pltpu.with_memory_space_constraint(r, pltpu.VMEM) for r in results))
     return (

time: 103 us -> 102 us (level)
  no operation moved by 1% of the time
where the time goes in v2:
time: 102 us
  Pallas kernels  101 us (99%)
    pallas_call x1, Pallas kernels, per_device(): pl.pallas_call(functools.partial(exchange_kernel, (seq_count, group_count...  97.8 us
    pallas_call x1, Pallas kernels, per_device(): pl.pallas_call(copy_out_kernel, out_shape=(jax.ShapeDtypeStruct((position...  3.36 us

profile of v2, /device:TPU:1, one launch (start us, length us, event | category | flops | bytes accessed | tf_op | source)
XLA Modules:
  0.0 101.8 jit_solution(2589449842625266937)
XLA Ops:
  0.6 97.8 %shard_map.85 = (bf16[64,3,128,128]{3,2,1,0:T(8,128)(2,1)S(1)}, bf16[64,128,128]{2,1,0:T(8,128)(2,1)S(1)}, s32[4,128]{1,0:T(4,128)S(1)}, bf16[2,4,32]{2,1,0:T(4,128)(2,1)S(1)}, bf16[1,1024]{1,0:T(2,128)(2,1)S(1)}) custom-call(s32[4]{0:T(128)} %lengths_in.1, s32[4,128]{1,0:T(4,128)} %table_in.1, bf16[4,64]{1,0:T(4,128)(2,1)} %bitcast.9, ...), custom_call_target="tpu_custom_call" | custom-call | tf_op jit(solution)/shard_map/pallas_call | solution.py:685
  98.4 3.4 %shard_map.86 = (bf16[64,4,128,128]{3,2,1,0:T(8,128)(2,1)}, bf16[2,4,32]{2,1,0:T(4,128)(2,1)}, bf16[1,1024]{1,0:T(2,128)(2,1)}) custom-call(bf16[64,3,128,128]{3,2,1,0:T(8,128)(2,1)S(1)} %get-tuple-element.11.placed_in, bf16[64,128,128]{2,1,0:T(8,128)(2,1)S(1)} %get-tuple-element.12.last_in, s32[4,128]{1,0:T(4,128)S(1)} %get-tuple-element.13.arrival_in, ...), custom_call_target="tpu_custom_call" | custom-call | tf_op jit(solution)/shard_map/pallas_call | solution.py:761

commit v3 on v2

--- a/solution.py
+++ b/solution.py
@@ -67,6 +67,8 @@
     word_sems,
     block_send,
     block_recv,
+    tail_blocks,
+    tail_sems,
     query_send,
     query_recv,
     scale_send,
@@ -223,6 +225,60 @@
     near_steps = [s for s in steps if (s // group_count).bit_count() <= 1]
     far_steps = [s for s in steps if s not in near_steps]
 
+    tail_plane, tail_step = planes - 1, far_steps[-1] if far_steps else 0
+    kept = capacity - tail_blocks.shape[0]
+    origin = (seq_count - 1) * group_count
+    to_relay = group_count * (1 << max(tail_step // group_count, 1).bit_length() - 1)
+    to_relay += tail_step % group_count
+    hands_over = me == origin
+    relays = me == origin ^ to_relay
+
+    def far_copy(plane, step):
+        if (plane, step) != (tail_plane, tail_step):
+            return block_copy(plane, step)
+        other = xor_index(me, step)
+        return pltpu.make_async_remote_copy(
+            src_ref=send.at[plane, other, pl.ds(0, kept)],
+            dst_ref=arrived[plane].at[pl.ds(me * capacity, kept)],
+            send_sem=block_send.at[plane, step],
+            recv_sem=block_recv.at[plane, step],
+            device_id=source_device(other),
+            device_id_type=MESH,
+        )
+
+    def tail_copy(source, owner, route, sent, received):
+        return pltpu.make_async_remote_copy(
+            src_ref=source,
+            dst_ref=arrived[tail_plane].at[
+                pl.ds(owner * capacity + kept, capacity - kept)
+            ],
+            send_sem=sent,
+            recv_sem=received,
+            device_id=source_device(xor_index(me, route)),
+            device_id_type=MESH,
+        )
+
+    if far_steps:
+        tail_source = send.at[tail_plane, xor_index(me, tail_step), pl.ds(kept, capacity - kept)]
+        tail_direct = tail_copy(
+            tail_source, me, tail_step, tail_sems.at[0], tail_sems.at[1]
+        )
+        tail_passed = tail_copy(
+            tail_blocks,
+            xor_index(me, to_relay),
+            tail_step ^ to_relay,
+            tail_sems.at[2],
+            tail_sems.at[1],
+        )
+        tail_handed = pltpu.make_async_remote_copy(
+            src_ref=tail_source,
+            dst_ref=tail_blocks,
+            send_sem=tail_sems.at[3],
+            recv_sem=tail_sems.at[4],
+            device_id=source_device(xor_index(me, to_relay)),
+            device_id_type=MESH,
+        )
+
     def picked(kind, other, within, request):
         group = other % group_count
         return pick_words[kind, within, group * per_group + request, other // group_count]
@@ -282,6 +338,8 @@
         sort_plane(plane)
         if plane == 1:
             send_plane(plane, near_steps)
+    if far_steps:
+        pl.when(hands_over)(tail_handed.start)
     for plane in range(planes):
         own_blocks(plane).start()
 
@@ -498,9 +556,20 @@
         att_copy(step).wait_recv()
     for plane in range(planes):
         for step in near_steps:
-            block_copy(plane, step).wait_send()
+            if step // group_count == 1:
+                block_copy(plane, step).wait_send()
+    if far_steps:
+
+        @pl.when(relays)
+        def _():
+            tail_handed.wait_recv()
+            tail_passed.start()
+
     for plane in range(planes):
-        send_plane(plane, far_steps)
+        for step in far_steps:
+            far_copy(plane, step).start()
+    if far_steps:
+        pl.when(jnp.logical_not(hands_over))(tail_direct.start)
 
     rows = sources * row_share
     gathered = attended[...].astype(f32).reshape(rows, head_size)
@@ -574,7 +643,7 @@
     for plane in range(planes - 1):
         own_blocks(plane).wait()
         for step in steps:
-            block_copy(plane, step).wait_recv()
+            (block_copy if step in near_steps else far_copy)(plane, step).wait_recv()
         for request in range(per_group):
 
             def place(turn, _):
@@ -598,9 +667,19 @@
         block_copy(planes - 1, step).wait_recv()
     for plane in range(planes):
         for step in far_steps:
-            block_copy(plane, step).wait_send()
+            far_copy(plane, step).wait_send()
+    for plane in range(planes):
+        for step in near_steps:
+            if step // group_count != 1:
+                block_copy(plane, step).wait_send()
+    if far_steps:
+        pl.when(hands_over)(tail_handed.wait_send)
+        pl.when(relays)(tail_passed.wait_send)
+        pl.when(jnp.logical_not(hands_over))(tail_direct.wait_send)
     for step in far_steps:
-        block_copy(planes - 1, step).wait_recv()
+        far_copy(planes - 1, step).wait_recv()
+    if far_steps:
+        tail_direct.wait_recv()
 
 
 def copy_out_kernel(
@@ -727,6 +806,8 @@
             dma((7 + key_heads * per_group,)),
             dma((planes, sources)),
             dma((planes, sources)),
+            pltpu.VMEM((max(capacity // 4, 1), block_size, head_size), bf16),
+            dma((5,)),
             dma((group_count,)),
             dma((group_count,)),
             dma((sources,)),

time: 102 us -> 101 us (level)
  no operation moved by 1% of the time
where the time goes in v3:
time: 101 us
  Pallas kernels  100 us (99%)
    pallas_call x1, Pallas kernels, per_device(): pl.pallas_call(functools.partial(exchange_kernel, (seq_count, group_count...  97.1 us
    pallas_call x1, Pallas kernels, per_device(): pl.pallas_call(copy_out_kernel, out_shape=(jax.ShapeDtypeStruct((position...  3.36 us

profile of v3, /device:TPU:1, one launch (start us, length us, event | category | flops | bytes accessed | tf_op | source)
XLA Modules:
  0.0 101.1 jit_solution(6469425874065380198)
XLA Ops:
  0.6 97.1 %shard_map.85 = (bf16[64,3,128,128]{3,2,1,0:T(8,128)(2,1)S(1)}, bf16[64,128,128]{2,1,0:T(8,128)(2,1)S(1)}, s32[4,128]{1,0:T(4,128)S(1)}, bf16[2,4,32]{2,1,0:T(4,128)(2,1)S(1)}, bf16[1,1024]{1,0:T(2,128)(2,1)S(1)}) custom-call(s32[4]{0:T(128)} %lengths_in.1, s32[4,128]{1,0:T(4,128)} %table_in.1, bf16[4,64]{1,0:T(4,128)(2,1)} %bitcast.9, ...), custom_call_target="tpu_custom_call" | custom-call | tf_op jit(solution)/shard_map/pallas_call | solution.py:764
  97.8 3.4 %shard_map.86 = (bf16[64,4,128,128]{3,2,1,0:T(8,128)(2,1)}, bf16[2,4,32]{2,1,0:T(4,128)(2,1)}, bf16[1,1024]{1,0:T(2,128)(2,1)}) custom-call(bf16[64,3,128,128]{3,2,1,0:T(8,128)(2,1)S(1)} %get-tuple-element.11.placed_in, bf16[64,128,128]{2,1,0:T(8,128)(2,1)S(1)} %get-tuple-element.12.last_in, s32[4,128]{1,0:T(4,128)S(1)} %get-tuple-element.13.arrival_in, ...), custom_call_target="tpu_custom_call" | custom-call | tf_op jit(solution)/shard_map/pallas_call | solution.py:842

commit v4 on v3

--- a/solution.py
+++ b/solution.py
@@ -62,6 +62,8 @@
     scale_words,
     arrival_words,
     pick_words,
+    slot_rows,
+    slot_words,
     load_sems,
     local_sems,
     word_sems,
@@ -165,19 +167,30 @@
     range_of = jnp.where(upper // share_blocks == lower, 1.0, 0.0).astype(bf16)
     own_rank = jnp.where(owner == me, ranks(owner == me), -1.0)
 
-    def pick(kind, values):
+    rank_rows = lax.broadcasted_iota(jnp.int32, (capacity, table_width), 0).astype(f32)
+    slots = jnp.zeros((capacity, table_width), f32)
+    for request in range(batch_rows):
+        column = upper // share_blocks + request // per_group * seq_count
+        slots += jnp.dot(
+            jnp.where(
+                own_rank[request : request + 1] == rank_rows, local[request : request + 1], 0.0
+            ).astype(bf16),
+            jnp.where(column == lower, 1.0, 0.0).astype(bf16),
+            preferred_element_type=f32,
+        )
+    slot_rows[...] = slots.astype(jnp.int32)
+    slot_copy = pltpu.make_async_copy(slot_rows, slot_words, word_sems.at[0])
+    slot_copy.start()
+
+    def pick(values):
         for within in range(capacity):
-            pick_rows[kind, within] = jnp.dot(
+            pick_rows[within] = jnp.dot(
                 jnp.where(own_rank == within, values, 0.0).astype(bf16),
                 range_of,
                 preferred_element_type=f32,
             ).astype(jnp.int32)
-        return pltpu.make_async_copy(
-            pick_rows.at[kind], pick_words.at[kind], word_sems.at[kind]
-        )
-
-    slot_copy = pick(0, local)
-    slot_copy.start()
+        return pltpu.make_async_copy(pick_rows, pick_words, word_sems.at[1])
+
     own_queries = pltpu.make_async_copy(queries_ref, all_queries.at[group_index], local_sems.at[0])
     pl.semaphore_wait(barrier, sources - 1 + jnp.where(below, 1, 0))
 
@@ -279,14 +292,12 @@
             device_id_type=MESH,
         )
 
-    def picked(kind, other, within, request):
+    def picked(other, within, request):
         group = other % group_count
-        return pick_words[kind, within, group * per_group + request, other // group_count]
+        return pick_words[within, group * per_group + request, other // group_count]
 
     def slot_of(other, within):
-        slot = picked(0, other, within, 0)
-        for request in range(1, per_group):
-            slot = slot + picked(0, other, within, request)
+        slot = slot_words[within, other % group_count * seq_count + other // group_count]
         return jnp.clip(slot, 0, pool_slots - 1)
 
     def sort_blocks(plane, other):
@@ -354,7 +365,7 @@
     live = jnp.clip(context - col_of * block_size, 0, block_size).astype(f32)
     scales_wide[...] = block_scale_ref[...].astype(f32)
     word_copies = [
-        pick(1, live),
+        pick(live),
         pltpu.make_async_copy(arrival_rows, arrival_words, word_sems.at[2]),
         pltpu.make_async_copy(scales_wide, scale_words, word_sems.at[3]),
     ]
@@ -387,10 +398,10 @@
             )
             highest = peaks[group]
             for within in range(capacity):
-                limit = jnp.full(lanes.shape, picked(1, other, within, 0), jnp.int32)
+                limit = jnp.full(lanes.shape, picked(other, within, 0), jnp.int32)
                 for request in range(1, per_group):
                     limit = jnp.where(
-                        row_ids >= request * groups, picked(1, other, within, request), limit
+                        row_ids >= request * groups, picked(other, within, request), limit
                     )
                 part = raw_scores[:, within * block_size : (within + 1) * block_size]
                 part = part * scale_words[2 * head, slot_of(other, within)] * root_scale
@@ -797,10 +808,12 @@
             pltpu.VMEM((tp_count, here, columns), f32),
             pltpu.VMEM((sources, planes, pool_slots), bf16),
             pltpu.VMEM((planes, pool_slots), f32),
-            pltpu.VMEM((2, capacity, batch_rows, table_width), jnp.int32),
+            pltpu.VMEM((capacity, batch_rows, table_width), jnp.int32),
             pltpu.SMEM((planes, pool_slots), f32),
             pltpu.SMEM((batch_rows, table_width), jnp.int32),
-            pltpu.SMEM((2, capacity, batch_rows, table_width), jnp.int32),
+            pltpu.SMEM((capacity, batch_rows, table_width), jnp.int32),
+            pltpu.VMEM((capacity, table_width), jnp.int32),
+            pltpu.SMEM((capacity, table_width), jnp.int32),
             dma((planes + 1,)),
             dma((planes + 3,)),
             dma((7 + key_heads * per_group,)),

time: 101 us -> 101 us (level)
  no operation moved by 1% of the time
where the time goes in v4:
time: 101 us
  Pallas kernels  100 us (99%)
    pallas_call x1, Pallas kernels, per_device(): pl.pallas_call(functools.partial(exchange_kernel, (seq_count, group_count...  96.9 us
    pallas_call x1, Pallas kernels, per_device(): pl.pallas_call(copy_out_kernel, out_shape=(jax.ShapeDtypeStruct((position...  3.36 us

profile of v4, /device:TPU:1, one launch (start us, length us, event | category | flops | bytes accessed | tf_op | source)
XLA Modules:
  0.0 100.9 jit_solution(6846089280201108288)
XLA Ops:
  0.6 96.9 %shard_map.85 = (bf16[64,3,128,128]{3,2,1,0:T(8,128)(2,1)S(1)}, bf16[64,128,128]{2,1,0:T(8,128)(2,1)S(1)}, s32[4,128]{1,0:T(4,128)S(1)}, bf16[2,4,32]{2,1,0:T(4,128)(2,1)S(1)}, bf16[1,1024]{1,0:T(2,128)(2,1)S(1)}) custom-call(s32[4]{0:T(128)} %lengths_in.1, s32[4,128]{1,0:T(4,128)} %table_in.1, bf16[4,64]{1,0:T(4,128)(2,1)} %bitcast.9, ...), custom_call_target="tpu_custom_call" | custom-call | tf_op jit(solution)/shard_map/pallas_call | solution.py:775
  97.6 3.4 %shard_map.86 = (bf16[64,4,128,128]{3,2,1,0:T(8,128)(2,1)}, bf16[2,4,32]{2,1,0:T(4,128)(2,1)}, bf16[1,1024]{1,0:T(2,128)(2,1)}) custom-call(bf16[64,3,128,128]{3,2,1,0:T(8,128)(2,1)S(1)} %get-tuple-element.11.placed_in, bf16[64,128,128]{2,1,0:T(8,128)(2,1)S(1)} %get-tuple-element.12.last_in, s32[4,128]{1,0:T(4,128)S(1)} %get-tuple-element.13.arrival_in, ...), custom_call_target="tpu_custom_call" | custom-call | tf_op jit(solution)/shard_map/pallas_call | solution.py:855

commit v5 on v4

--- a/solution.py
+++ b/solution.py
@@ -444,7 +444,7 @@
                 for piece in range(per_tile):
                     low = request * groups + piece * row_share
                     place = tile * per_tile + piece
-                    parts[place] = accums[group, low : low + row_share].astype(bf16)
+                    parts[place] = accums[group, low : low + row_share]
                     stats[place] = jnp.sum(
                         jnp.where(
                             share_lanes == share_rows, peaks[group, low : low + row_share], 0.0
@@ -544,7 +544,7 @@
     denominator = jnp.zeros_like(highest)
     for source in range(sources):
         factor = jnp.exp(source_peaks[source] - highest)
-        numerator += parts_in[source].astype(f32) * factor
+        numerator += parts_in[source] * factor
         denominator += spread(source, row_share) * factor
     attended[me] = (numerator / denominator).astype(jnp.bfloat16)
 
@@ -799,8 +799,8 @@
             pltpu.VMEM((group_count, query_rows, block_size), f32),
             pltpu.VMEM((group_count, query_rows, block_size), f32),
             pltpu.VMEM((group_count, query_rows, head_size), f32),
-            pltpu.VMEM((sources, row_share, head_size), bf16),
-            pltpu.VMEM((sources, row_share, head_size), bf16),
+            pltpu.VMEM((sources, row_share, head_size), f32),
+            pltpu.VMEM((sources, row_share, head_size), f32),
             pltpu.VMEM((sources, 1, head_size), f32),
             pltpu.VMEM((sources, 1, head_size), f32),
             pltpu.VMEM((sources, row_share, head_size), bf16),

time: 101 us -> 101 us (level)
  no operation moved by 1% of the time
where the time goes in v5:
time: 101 us
  Pallas kernels  100 us (99%)
    pallas_call x1, Pallas kernels, per_device(): pl.pallas_call(functools.partial(exchange_kernel, (seq_count, group_count...  97.1 us
    pallas_call x1, Pallas kernels, per_device(): pl.pallas_call(copy_out_kernel, out_shape=(jax.ShapeDtypeStruct((position...  3.36 us

profile of v5, /device:TPU:1, one launch (start us, length us, event | category | flops | bytes accessed | tf_op | source)
XLA Modules:
  0.0 101.1 jit_solution(11560302310153286522)
XLA Ops:
  0.6 97.1 %shard_map.85 = (bf16[64,3,128,128]{3,2,1,0:T(8,128)(2,1)S(1)}, bf16[64,128,128]{2,1,0:T(8,128)(2,1)S(1)}, s32[4,128]{1,0:T(4,128)S(1)}, bf16[2,4,32]{2,1,0:T(4,128)(2,1)S(1)}, bf16[1,1024]{1,0:T(2,128)(2,1)S(1)}) custom-call(s32[4]{0:T(128)} %lengths_in.1, s32[4,128]{1,0:T(4,128)} %table_in.1, bf16[4,64]{1,0:T(4,128)(2,1)} %bitcast.9, ...), custom_call_target="tpu_custom_call" | custom-call | tf_op jit(solution)/shard_map/pallas_call | solution.py:775
  97.7 3.4 %shard_map.86 = (bf16[64,4,128,128]{3,2,1,0:T(8,128)(2,1)}, bf16[2,4,32]{2,1,0:T(4,128)(2,1)}, bf16[1,1024]{1,0:T(2,128)(2,1)}) custom-call(bf16[64,3,128,128]{3,2,1,0:T(8,128)(2,1)S(1)} %get-tuple-element.11.placed_in, bf16[64,128,128]{2,1,0:T(8,128)(2,1)S(1)} %get-tuple-element.12.last_in, s32[4,128]{1,0:T(4,128)S(1)} %get-tuple-element.13.arrival_in, ...), custom_call_target="tpu_custom_call" | custom-call | tf_op jit(solution)/shard_map/pallas_call | solution.py:855

commit v6 on v5

--- a/solution.py
+++ b/solution.py
@@ -128,7 +128,7 @@
         return {"seq": other // group_count, "grp": other % group_count}
 
     barrier = pltpu.get_barrier_semaphore()
-    for step in range(1, sources):
+    for step in reversed(range(1, sources)):
         pl.semaphore_signal(
             barrier, inc=1, device_id=source_device(xor_index(me, step)), device_id_type=MESH
         )
@@ -243,8 +243,8 @@
     origin = (seq_count - 1) * group_count
     to_relay = group_count * (1 << max(tail_step // group_count, 1).bit_length() - 1)
     to_relay += tail_step % group_count
-    hands_over = me == origin
-    relays = me == origin ^ to_relay
+    hands_over = seq_index == seq_count - 1
+    relays = seq_index == (seq_count - 1) ^ (to_relay // group_count)
 
     def far_copy(plane, step):
         if (plane, step) != (tail_plane, tail_step):
@@ -819,7 +819,7 @@
             dma((7 + key_heads * per_group,)),
             dma((planes, sources)),
             dma((planes, sources)),
-            pltpu.VMEM((max(capacity // 4, 1), block_size, head_size), bf16),
+            pltpu.VMEM((max(capacity // 8, 1), block_size, head_size), bf16),
             dma((5,)),
             dma((group_count,)),
             dma((group_count,)),

time: 101 us -> 101 us (level)
  no operation moved by 1% of the time
where the time goes in v6:
time: 101 us
  Pallas kernels  100 us (99%)
    pallas_call x1, Pallas kernels, per_device(): pl.pallas_call(functools.partial(exchange_kernel, (seq_count, group_count...  97.1 us
    pallas_call x1, Pallas kernels, per_device(): pl.pallas_call(copy_out_kernel, out_shape=(jax.ShapeDtypeStruct((position...  3.36 us

profile of v6, /device:TPU:1, one launch (start us, length us, event | category | flops | bytes accessed | tf_op | source)
XLA Modules:
  0.0 101.1 jit_solution(14357247164771961714)
XLA Ops:
  0.6 97.1 %shard_map.85 = (bf16[64,3,128,128]{3,2,1,0:T(8,128)(2,1)S(1)}, bf16[64,128,128]{2,1,0:T(8,128)(2,1)S(1)}, s32[4,128]{1,0:T(4,128)S(1)}, bf16[2,4,32]{2,1,0:T(4,128)(2,1)S(1)}, bf16[1,1024]{1,0:T(2,128)(2,1)S(1)}) custom-call(s32[4]{0:T(128)} %lengths_in.1, s32[4,128]{1,0:T(4,128)} %table_in.1, bf16[4,64]{1,0:T(4,128)(2,1)} %bitcast.9, ...), custom_call_target="tpu_custom_call" | custom-call | tf_op jit(solution)/shard_map/pallas_call | solution.py:775
  97.7 3.4 %shard_map.86 = (bf16[64,4,128,128]{3,2,1,0:T(8,128)(2,1)}, bf16[2,4,32]{2,1,0:T(4,128)(2,1)}, bf16[1,1024]{1,0:T(2,128)(2,1)}) custom-call(bf16[64,3,128,128]{3,2,1,0:T(8,128)(2,1)S(1)} %get-tuple-element.11.placed_in, bf16[64,128,128]{2,1,0:T(8,128)(2,1)S(1)} %get-tuple-element.12.last_in, s32[4,128]{1,0:T(4,128)S(1)} %get-tuple-element.13.arrival_in, ...), custom_call_target="tpu_custom_call" | custom-call | tf_op jit(solution)/shard_map/pallas_call | solution.py:855
